TPU v7x, 32 devices: a whole 2x2x4 slice. The times are simulated.
32 devices in a mesh: owner: 4 (over y, core), rows: 8 (over z, x).
Axes of the slice: x: 2, y: 2, z: 4, core: 2. Of those that a mesh axis runs over, the one named last changes fastest.
Arguments:
- train_gate: float32 [128, 2048, 768], P('owner', 'rows'), may hold values from -0.125 to 0.125
- train_up: float32 [128, 2048, 768], P('owner', 'rows'), may hold values from -0.125 to 0.125
- router_weight: float32 [2048, 128], P('rows', 'owner'), may hold values from -0.125 to 0.125
- router_gain: float32 [2048], P('rows'), may hold values from 0.25 to 1.75
Outputs:
- ready_gate: bfloat16 [128, 768, 2048], P(('owner', 'rows'))
- ready_up: bfloat16 [128, 768, 2048], P(('owner', 'rows'))
- serve_router: bfloat16 [2048, 128], replicated
All inputs are finite; a program needn't handle non-finite values.
Results may differ from a plain program's by a relative error of at most 0.001.
Values may be sent and summed in bfloat16 or wider, within the bound.
A program may use at most 192 MiB of HBM per device.

v0:
```python
import jax
import jax.numpy as jnp
from jax import lax
from jax.sharding import PartitionSpec as P


def on_device(train_gate, train_up, router_weight, router_gain):
    narrow_gate, narrow_up = (train_gate.astype(jnp.bfloat16), train_up.astype(jnp.bfloat16))
    ready_gate, ready_up = (
        lax.all_to_all(narrow_gate, "rows", split_axis=0, concat_axis=1, tiled=True),
        lax.all_to_all(narrow_up, "rows", split_axis=0, concat_axis=1, tiled=True),
    )
    ready_gate = jnp.transpose(ready_gate, (0, 2, 1))
    ready_up = jnp.transpose(ready_up, (0, 2, 1))
    part_router = (router_weight * router_gain[:, None]).astype(jnp.bfloat16)
    row_router = lax.all_gather(part_router, "rows", axis=0, tiled=True)
    serve_router = lax.all_gather(row_router, "owner", axis=1, tiled=True)
    return (ready_gate, ready_up, serve_router)


def solution(mesh):
    placed = (P("owner", "rows", None), P("owner", "rows", None), P("rows", "owner"), P("rows"))
    return jax.shard_map(
        on_device,
        mesh=mesh,
        in_specs=placed,
        out_specs=(P(("owner", "rows"), None, None), P(("owner", "rows"), None, None), P()),
        check_vma=False,
    )
```

profile of v0, /device:TPU:0, one launch (start us, length us, event | category | flops | bytes accessed | tf_op | source)
XLA Modules:
  0.0 672.7 jit_solution(13268045616997217038)
XLA Ops:
  0.6 13.2 %convert_element_type.9 = bf16[32,256,768]{2,1,0:T(8,128)(2,1)} convert(f32[32,256,768]{2,1,0:T(8,128)} %param.4) | non-fusion elementwise | flops 6291456 | bytes 37748736 | tf_op jit(solution)/shard_map/convert_element_type | solution.py:8
  13.8 7.3 %all-to-all-start = ((bf16[32,256,768]{2,1,0:T(8,128)(2,1)}), bf16[32,256,768]{2,1,0:T(8,128)(2,1)}, u32[]{:S(2)}, u32[]{:S(2)}) async-start(bf16[32,256,768]{2,1,0:T(8,128)(2,1)} %convert_element_type.9), calls=%async_computation | async-start | bytes 25165824 | tf_op jit(solution)/shard_map/all_to_all | solution.py:10
  21.1 13.4 %convert_element_type.10 = bf16[32,256,768]{2,1,0:T(8,128)(2,1)} convert(f32[32,256,768]{2,1,0:T(8,128)} %param.5) | non-fusion elementwise | flops 6291456 | bytes 37748736 | tf_op jit(solution)/shard_map/convert_element_type | solution.py:8
  34.5 0.0 copy-start
  34.5 0.0 copy-start.1
  34.5 259.7 %all-to-all-done = bf16[32,256,768]{2,1,0:T(8,128)(2,1)} async-done(((bf16[32,256,768]{2,1,0:T(8,128)(2,1)}), bf16[32,256,768]{2,1,0:T(8,128)(2,1)}, u32[]{:S(2)}, u32[]{:S(2)}) %all-to-all-start) | async-done | bytes 12582944 | tf_op jit(solution)/shard_map/all_to_all | solution.py:10
  294.2 5.3 all-to-all-start.1
  299.5 0.0 copy-done
  299.5 0.0 copy-done.1
  299.5 292.2 %all_gather.6 = bf16[2048,32]{0,1:T(8,128)(2,1)S(1)} all-gather(bf16[256,32]{0,1:T(8,128)(2,1)S(1)} %multiply_convert_fusion), channel_id=1, replica_groups=mesh['owner'=4,'rows'=8] {'rows'}, dimensions={0}, use_global_device_ids=true | all-gather | bytes 147456 | tf_op jit(solution)/shard_map/all_gather | solution.py:16
  591.8 7.2 %all_gather.7 = bf16[2048,128]{0,1:T(8,128)(2,1)S(1)} all-gather(bf16[2048,32]{0,1:T(8,128)(2,1)S(1)} %all_gather.6), channel_id=1, replica_groups=mesh['owner'=4,'rows'=8] {'owner'}, dimensions={1}, use_global_device_ids=true | all-gather | bytes 655360 | tf_op jit(solution)/shard_map/all_gather | solution.py:17
  598.9 1.0 copy.12
  599.9 16.9 %copy.10 = bf16[8,4,256,768]{2,0,3,1:T(8,128)(2,1)} copy(bf16[8,4,256,768]{3,2,1,0:T(8,128)(2,1)} %bitcast) | data formatting | bytes 25165824 | tf_op jit(solution)/shard_map/all_to_all | solution.py:10
  616.8 19.5 %all_to_all.29 = bf16[4,2048,768]{1,2,0:T(8,128)(2,1)} reshape(bf16[4,8,256,768]{2,1,3,0:T(8,128)(2,1)} %bitcast.14) | data formatting | bytes 25165824 | tf_op jit(solution)/shard_map/all_to_all | solution.py:10
  636.3 0.0 all-to-all-done.1
  636.3 16.9 %copy.11 = bf16[8,4,256,768]{2,0,3,1:T(8,128)(2,1)} copy(bf16[8,4,256,768]{3,2,1,0:T(8,128)(2,1)} %bitcast.3) | data formatting | bytes 25165824 | tf_op jit(solution)/shard_map/all_to_all | solution.py:11
  653.2 19.5 %all_to_all.33 = bf16[4,2048,768]{1,2,0:T(8,128)(2,1)} reshape(bf16[4,8,256,768]{2,1,3,0:T(8,128)(2,1)} %bitcast.15) | data formatting | bytes 25165824 | tf_op jit(solution)/shard_map/all_to_all | solution.py:11
  (1 shorter events, 0.0 us)
Async XLA Ops:
  13.8 280.3 %all-to-all-start = ((bf16[32,256,768]{2,1,0:T(8,128)(2,1)}), bf16[32,256,768]{2,1,0:T(8,128)(2,1)}, u32[]{:S(2)}, u32[]{:S(2)}) async-start(bf16[32,256,768]{2,1,0:T(8,128)(2,1)} %convert_element_type.9), calls=%async_computation | async-start | bytes 25165824 | tf_op jit(solution)/shard_map/all_to_all | solution.py:10
  34.5 265.0 %copy-start = (f32[256,32]{0,1:T(8,128)S(1)}, f32[256,32]{0,1:T(8,128)}, u32[]{:S(2)}) copy-start(f32[256,32]{0,1:T(8,128)} %param.6) | copy-start | bytes 98308
  34.5 265.0 %copy-start.1 = (f32[256]{0:T(256)S(1)}, f32[256]{0:T(256)}, u32[]{:S(2)}) copy-start(f32[256]{0:T(256)} %param.7) | copy-start | bytes 3076
  294.2 342.1 %all-to-all-start.1 = ((bf16[32,256,768]{2,1,0:T(8,128)(2,1)}), bf16[32,256,768]{2,1,0:T(8,128)(2,1)}, u32[]{:S(2)}, u32[]{:S(2)}) async-start(bf16[32,256,768]{2,1,0:T(8,128)(2,1)} %convert_element_type.10), calls=%async_computation.1 | async-start | bytes 25165824 | tf_op jit(solution)/shard_map/all_to_all | solution.py:11
where the time goes:
time: 675 us; the launch traced here: 673 us
  blocking collectives  299 us (44%)
  waiting for transfers between devices  260 us (39%)
  local copies, waits for them, and re-layouts  73.7 us (11%)
  other arithmetic  26.6 us (4%)
  starting transfers between devices  12.6 us (2%)
    all_gather x1, blocking collectives, on_device(): row_router = lax.all_gather(part_router, 'rows', axis=0, tiled=True)  292 us
    all_to_all x1, waiting for transfers between devices, on_device(): lax.all_to_all(narrow_gate, 'rows', split_axis=0, concat_axis=1, tiled=True)  260 us
    all_to_all x2, local copies, waits for them, and re-layouts, on_device(): lax.all_to_all(narrow_up, 'rows', split_axis=0, concat_axis=1, tiled=True)  36.4 us
    all_to_all x2, local copies, waits for them, and re-layouts, on_device(): lax.all_to_all(narrow_gate, 'rows', split_axis=0, concat_axis=1, tiled=True)  36.3 us
  transfers between devices with their start and end apart: 2, of which 1 were waited for; matrix products, arithmetic and copies ran while one was open for 5% of the time, Pallas kernels for 0%

commit v1 on v0

--- a/solution.py
+++ b/solution.py
@@ -4,10 +4,33 @@
 from jax.sharding import PartitionSpec as P
 
 
+def cut_along(shard, dim, size):
+    dims = shard.shape
+    blocks = shard.reshape(*dims[:dim], size, dims[dim] // size, *dims[dim + 1 :])
+    return jnp.moveaxis(blocks, dim, 0)
+
+
+def laid_out(blocks, dim):
+    shape = list(blocks.shape[1:])
+    shape[dim] *= blocks.shape[0]
+    return jnp.moveaxis(blocks, 0, dim).reshape(shape)
+
+
+def sent_to_each(x, axis, split_dim, concat_dim):
+    devices, index = (lax.axis_size(axis), lax.axis_index(axis))
+    tiles = cut_along(x, split_dim, devices)
+    outs = [tiles[index]]
+    for step in range(1, devices):
+        sent = tiles[(index + step) % devices]
+        outs.append(lax.ppermute(sent, axis, [(i, (i + step) % devices) for i in range(devices)]))
+    tiles = jnp.stack(outs)[(index - jnp.arange(devices)) % devices]
+    return laid_out(tiles, concat_dim)
+
+
 def on_device(train_gate, train_up, router_weight, router_gain):
     narrow_gate, narrow_up = (train_gate.astype(jnp.bfloat16), train_up.astype(jnp.bfloat16))
     ready_gate, ready_up = (
-        lax.all_to_all(narrow_gate, "rows", split_axis=0, concat_axis=1, tiled=True),
+        sent_to_each(narrow_gate, "rows", 0, 1),
         lax.all_to_all(narrow_up, "rows", split_axis=0, concat_axis=1, tiled=True),
     )
     ready_gate = jnp.transpose(ready_gate, (0, 2, 1))

time: 675 us -> 705 us (1.044)
  waiting for transfers between devices: 260 us -> 52.7 us
  blocking collectives: 299 us -> 505 us
  local copies, waits for them, and re-layouts: 73.7 us -> 101 us
    all_to_all x1 -> x0, waiting for transfers between devices: 260 us -> none  [on_device(): lax.all_to_all(narrow_gate, 'rows', split_axis=0, concat_axis=1, tiled=True)]
    all_gather x1, blocking collectives: 292 us -> 497 us  [on_device(): row_router = lax.all_gather(part_router, 'rows', axis=0, tiled=True)]
    ppermute x0 -> x7, waiting for transfers between devices: none -> 52.7 us  [sent_to_each(): lax.ppermute(sent, axis, [(i, (i + step) % devices) for i in range(device...]
    all_to_all x2 -> x0, local copies, waits for them, and re-layouts: 36.3 us -> none  [on_device(): lax.all_to_all(narrow_gate, 'rows', split_axis=0, concat_axis=1, tiled=True)]
    unnamed x5 -> x12, local copies, waits for them, and re-layouts: 1.01 us -> 32.1 us
    gather x0 -> x1, local copies, waits for them, and re-layouts: none -> 11.2 us  [sent_to_each(): tiles = jnp.stack(outs)[(index - jnp.arange(devices)) % devices]]
    transpose x0 -> x1, local copies, waits for them, and re-layouts: none -> 10.8 us  [laid_out(): return jnp.moveaxis(blocks, 0, dim).reshape(shape)]
    ppermute x0 -> x7, starting transfers between devices: none -> 10.3 us  [sent_to_each(): lax.ppermute(sent, axis, [(i, (i + step) % devices) for i in range(device...]
  transfers between devices with their start and end apart: 2 -> 8, of which waited for: 1 -> 2; matrix products, arithmetic and copies ran while one was open for 5% -> 11% of each run, Pallas kernels for 0% -> 0%
where the time goes in v1:
time: 705 us; the launch traced here: 703 us
  blocking collectives  505 us (72%)
  local copies, waits for them, and re-layouts  101 us (14%)
  waiting for transfers between devices  52.7 us (7%)
  other arithmetic  26.5 us (4%)
  starting transfers between devices  17.6 us (2%)
    all_gather x1, blocking collectives, on_device(): row_router = lax.all_gather(part_router, 'rows', axis=0, tiled=True)  497 us
    ppermute x7, waiting for transfers between devices, sent_to_each(): lax.ppermute(sent, axis, [(i, (i + step) % devices) for i in range(device...  52.7 us
    all_to_all x2, local copies, waits for them, and re-layouts, on_device(): lax.all_to_all(narrow_up, 'rows', split_axis=0, concat_axis=1, tiled=True)  36.4 us
    unnamed x12, local copies, waits for them, and re-layouts  32.1 us
  transfers between devices with their start and end apart: 8, of which 2 were waited for; matrix products, arithmetic and copies ran while one was open for 11% of the time, Pallas kernels for 0%

profile of v1, /device:TPU:0, one launch (start us, length us, event | category | flops | bytes accessed | tf_op | source)
XLA Modules:
  0.0 702.9 jit_solution(16116264633652682472)
XLA Ops:
  0.6 13.3 %convert_element_type.10 = bf16[32,256,768]{2,1,0:T(8,128)(2,1)} convert(f32[32,256,768]{2,1,0:T(8,128)} %param.5) | non-fusion elementwise | flops 6291456 | bytes 37748736 | tf_op jit(solution)/shard_map/convert_element_type | solution.py:31
  14.0 7.3 %all-to-all-start = ((bf16[32,256,768]{2,1,0:T(8,128)(2,1)}), bf16[32,256,768]{2,1,0:T(8,128)(2,1)}, u32[]{:S(2)}, u32[]{:S(2)}) async-start(bf16[32,256,768]{2,1,0:T(8,128)(2,1)} %convert_element_type.10), calls=%async_computation | async-start | bytes 25165824 | tf_op jit(solution)/shard_map/all_to_all | solution.py:34
  21.2 13.2 %convert_element_type.9 = bf16[32,256,768]{2,1,0:T(8,128)(2,1)} convert(f32[32,256,768]{2,1,0:T(8,128)} %param.4) | non-fusion elementwise | flops 6291456 | bytes 37748736 | tf_op jit(solution)/shard_map/convert_element_type | solution.py:31
  34.4 9.1 %dynamic-slice_bitcast_fusion = (bf16[4,256,768]{2,1,0:T(8,128)(2,1)}, bf16[4,256,768]{2,1,0:T(8,128)(2,1)}, bf16[4,256,768]{2,1,0:T(8,128)(2,1)}, bf16[4,256,76...) fusion(bf16[8,4,256,768]{3,2,1,0:T(8,128)(2,1)} %bitcast.45, ...), kind=kLoop, calls=%fused_computation.8 | loop fusion | bytes 25165856 | tf_op jit(solution)/shard_map/squeeze | solution.py:24
  43.5 2.1 collective-permute-start
  45.6 1.5 collective-permute-start.1
  47.0 2.4 collective-permute-start.2
  49.4 1.5 collective-permute-start.3
  50.9 2.4 collective-permute-start.4
  53.3 497.4 %all_gather.6 = bf16[2048,32]{0,1:T(8,128)(2,1)S(1)} all-gather(bf16[256,32]{0,1:T(8,128)(2,1)S(1)} %multiply_convert_fusion), channel_id=1, replica_groups=mesh['owner'=4,'rows'=8] {'rows'}, dimensions={0}, use_global_device_ids=true | all-gather | bytes 147456 | tf_op jit(solution)/shard_map/all_gather | solution.py:39
  550.7 7.2 %all_gather.7 = bf16[2048,128]{0,1:T(8,128)(2,1)S(1)} all-gather(bf16[2048,32]{0,1:T(8,128)(2,1)S(1)} %all_gather.6), channel_id=1, replica_groups=mesh['owner'=4,'rows'=8] {'owner'}, dimensions={1}, use_global_device_ids=true | all-gather | bytes 655360 | tf_op jit(solution)/shard_map/all_gather | solution.py:40
  559.5 2.7 bitcast_dynamic-update-slice_fusion.6
  562.1 2.7 bitcast_dynamic-update-slice_fusion.5
  564.8 2.7 bitcast_dynamic-update-slice_fusion.4
  567.4 2.7 bitcast_dynamic-update-slice_fusion.3
  570.1 1.2 bitcast_dynamic-update-slice_fusion.2
  571.3 24.1 %collective-permute-done.5 = bf16[4,256,768]{2,1,0:T(8,128)(2,1)} collective-permute-done((bf16[4,256,768]{2,1,0:T(8,128)(2,1)}, bf16[4,256,768]{2,1,0:T(8,128)(2,1)}, u32[]{:S(2)}, u32[]{:S(2)}) %collective-permute-start.5) | collective-permute-done | bytes 1572896 | tf_op jit(solution)/shard_map/ppermute | solution.py:25
  595.5 2.7 bitcast_dynamic-update-slice_fusion.1
  598.1 28.5 %collective-permute-done.6 = bf16[4,256,768]{2,1,0:T(8,128)(2,1)S(1)} collective-permute-done((bf16[4,256,768]{2,1,0:T(8,128)(2,1)}, bf16[4,256,768]{2,1,0:T(8,128)(2,1)S(1)}, u32[]{:S(2)}, u32[]{:S(2)}) %collective-permute-start.6) | collective-permute-done | bytes 1572896 | tf_op jit(solution)/shard_map/ppermute | solution.py:25
  627.9 11.2 %gather_fusion = bf16[8,4,256,768]{3,2,1,0:T(8,128)(2,1)} fusion(bf16[8,4,256,768]{3,2,1,0:T(8,128)(2,1)} %bitcast_dynamic-update-slice_fusion, s32[1024]{0:T(1024)S(1)} %pad_clamp_fusion), kind=kCustom, calls=%fused_computation | custom fusion | bytes 25165856 | tf_op jit(solution)/shard_map/gather | solution.py:26
  639.1 10.8 %copy.15 = bf16[4,8,256,768]{3,2,1,0:T(8,128)(2,1)} copy(bf16[4,8,256,768]{3,2,0,1:T(8,128)(2,1)} %bitcast.44) | data formatting | bytes 25165824 | tf_op jit(solution)/shard_map/transpose | solution.py:16
  649.9 16.6 %copy.17 = bf16[4,768,2048]{2,1,0:T(8,128)(2,1)} copy(bf16[4,768,2048]{1,2,0:T(8,128)(2,1)} %bitcast.42) | data formatting | bytes 25165824
  666.6 16.9 %copy.16 = bf16[8,4,256,768]{2,0,3,1:T(8,128)(2,1)} copy(bf16[8,4,256,768]{3,2,1,0:T(8,128)(2,1)} %bitcast.19) | data formatting | bytes 25165824 | tf_op jit(solution)/shard_map/all_to_all | solution.py:34
  683.4 19.5 %all_to_all.16 = bf16[4,2048,768]{1,2,0:T(8,128)(2,1)} reshape(bf16[4,8,256,768]{2,1,3,0:T(8,128)(2,1)} %bitcast.43) | data formatting | bytes 25165824 | tf_op jit(solution)/shard_map/all_to_all | solution.py:34
  (17 shorter events, 2.9 us)
Async XLA Ops:
  14.0 652.6 %all-to-all-start = ((bf16[32,256,768]{2,1,0:T(8,128)(2,1)}), bf16[32,256,768]{2,1,0:T(8,128)(2,1)}, u32[]{:S(2)}, u32[]{:S(2)}) async-start(bf16[32,256,768]{2,1,0:T(8,128)(2,1)} %convert_element_type.10), calls=%async_computation | async-start | bytes 25165824 | tf_op jit(solution)/shard_map/all_to_all | solution.py:34
  34.4 18.8 %copy-start = (f32[256,32]{0,1:T(8,128)S(1)}, f32[256,32]{0,1:T(8,128)}, u32[]{:S(2)}) copy-start(f32[256,32]{0,1:T(8,128)} %param.6) | copy-start | bytes 98308
  34.4 18.8 %copy-start.1 = (f32[256]{0:T(256)S(1)}, f32[256]{0:T(256)}, u32[]{:S(2)}) copy-start(f32[256]{0:T(256)} %param.7) | copy-start | bytes 3076
  43.5 514.4 %collective-permute-start = (bf16[4,256,768]{2,1,0:T(8,128)(2,1)S(1)}, bf16[4,256,768]{2,1,0:T(8,128)(2,1)}, u32[]{:S(2)}, u32[]{:S(2)}) collective-permute-start(bf16[4,256,768]{2,1,0:T(8,128)(2,1)S(1)} %get-tuple-element.15), channel_id=1, source_target_pairs={{0,1},{1,2},{2,3},{3,4},{4,5},{5,6},{6,7},{7,0},{8,9},{9,10},{10,1... | collective-permute-start | bytes 4718600 | tf_op jit(solution)/shard_map/ppermute | solution.py:25
  45.6 513.9 %collective-permute-start.1 = (bf16[4,256,768]{2,1,0:T(8,128)(2,1)}, bf16[4,256,768]{2,1,0:T(8,128)(2,1)}, u32[]{:S(2)}, u32[]{:S(2)}) collective-permute-start(bf16[4,256,768]{2,1,0:T(8,128)(2,1)} %get-tuple-element.14), channel_id=1, source_target_pairs={{0,2},{1,3},{2,4},{3,5},{4,6},{5,7},{6,0},{7,1},{8,10},{9,11},{10,... | collective-permute-start | bytes 4718600 | tf_op jit(solution)/shard_map/ppermute | solution.py:25
  47.0 517.7 %collective-permute-start.2 = (bf16[4,256,768]{2,1,0:T(8,128)(2,1)}, bf16[4,256,768]{2,1,0:T(8,128)(2,1)}, u32[]{:S(2)}, u32[]{:S(2)}) collective-permute-start(bf16[4,256,768]{2,1,0:T(8,128)(2,1)} %get-tuple-element.13), channel_id=1, source_target_pairs={{0,3},{1,4},{2,5},{3,6},{4,7},{5,0},{6,1},{7,2},{8,11},{9,12},{10,... | collective-permute-start | bytes 4718600 | tf_op jit(solution)/shard_map/ppermute | solution.py:25
  49.4 518.0 %collective-permute-start.3 = (bf16[4,256,768]{2,1,0:T(8,128)(2,1)}, bf16[4,256,768]{2,1,0:T(8,128)(2,1)}, u32[]{:S(2)}, u32[]{:S(2)}) collective-permute-start(bf16[4,256,768]{2,1,0:T(8,128)(2,1)} %get-tuple-element.12), channel_id=1, source_target_pairs={{0,4},{1,5},{2,6},{3,7},{4,0},{5,1},{6,2},{7,3},{8,12},{9,13},{10,... | collective-permute-start | bytes 4718600 | tf_op jit(solution)/shard_map/ppermute | solution.py:25
  50.9 519.2 %collective-permute-start.4 = (bf16[4,256,768]{2,1,0:T(8,128)(2,1)}, bf16[4,256,768]{2,1,0:T(8,128)(2,1)S(1)}, u32[]{:S(2)}, u32[]{:S(2)}) collective-permute-start(bf16[4,256,768]{2,1,0:T(8,128)(2,1)} %get-tuple-element.11), channel_id=1, source_target_pairs={{0,5},{1,6},{2,7},{3,0},{4,1},{5,2},{6,3},{7,4},{8,13},{9,14},{10,... | collective-permute-start | bytes 4718600 | tf_op jit(solution)/shard_map/ppermute | solution.py:25
  557.9 37.6 %collective-permute-start.5 = (bf16[4,256,768]{2,1,0:T(8,128)(2,1)}, bf16[4,256,768]{2,1,0:T(8,128)(2,1)}, u32[]{:S(2)}, u32[]{:S(2)}) collective-permute-start(bf16[4,256,768]{2,1,0:T(8,128)(2,1)} %get-tuple-element.10), channel_id=1, source_target_pairs={{0,6},{1,7},{2,0},{3,1},{4,2},{5,3},{6,4},{7,5},{8,14},{9,15},{10,... | collective-permute-start | bytes 4718600 | tf_op jit(solution)/shard_map/ppermute | solution.py:25
  559.5 67.2 %collective-permute-start.6 = (bf16[4,256,768]{2,1,0:T(8,128)(2,1)}, bf16[4,256,768]{2,1,0:T(8,128)(2,1)S(1)}, u32[]{:S(2)}, u32[]{:S(2)}) collective-permute-start(bf16[4,256,768]{2,1,0:T(8,128)(2,1)} %get-tuple-element.9), channel_id=1, source_target_pairs={{0,7},{1,0},{2,1},{3,2},{4,3},{5,4},{6,5},{7,6},{8,15},{9,8},{10,9... | collective-permute-start | bytes 4718600 | tf_op jit(solution)/shard_map/ppermute | solution.py:25
